TPU v7x, 256 devices: a whole 4x4x8 slice. The times are simulated.
256 devices in a mesh: seq: 2 (over core), chan: 16 (over y, x), batch: 8 (over z).
Axes of the slice: x: 4, y: 4, z: 8, core: 2. Of those that a mesh axis runs over, the one named last changes fastest.
Arguments:
- ssm_input: bfloat16 [16384, 4096], P(('batch', 'seq'), 'chan'), parts along dimension 0, may hold values from -6 to 6
- gate_z: bfloat16 [16384, 4096], P(('batch', 'seq'), 'chan'), parts along dimension 0, may hold values from -6 to 6
- proj_forward: bfloat16 [2, 16384, 128], P(None, ('batch', 'seq')), parts along dimension 1, may hold values from -2 to 2
- proj_backward: bfloat16 [2, 16384, 128], P(None, ('batch', 'seq')), parts along dimension 1, may hold values from -2 to 2
- step_raw: float32 [2, 64, 16384], P(None, 'chan', ('batch', 'seq')), parts along dimension 2, may hold values from -3 to 3
- head_params: float32 [2, 2, 64], P(None, None, 'chan'), may hold values from -4 to 1, as said below
- skip_gain: float32 [64], P('chan'), may hold values from 0.25 to 2
- norm_gain: float32 [4096], P('chan'), may hold values from 0.5 to 1.5
- out_weight: bfloat16 [4096, 2048], P(None, 'chan'), may hold values from -0.09375 to 0.09375
Outputs:
- mixed: bfloat16 [16384, 2048], P(('batch', 'seq'), 'chan'), parts along dimension 0
There are 8 independent parts, one for each index of `batch`. A program takes and returns all parts, laid end to end along the dimension named above; an argument that names none is the same for every part. Nothing has to cross between parts.
Inputs may be any that keep to these rules, and one draw needn't show every extreme that they name: `head_params`: index 0 of the second dimension holds positive decay rates, index 1 time-step biases.
All inputs are finite; a program needn't handle non-finite values.
Results may differ from a plain program's by a relative error of at most 0.0085.
Values may be sent and summed in bfloat16 or wider, within the bound.
A program may use at most 128 MiB of HBM per device.

v0:
```python
import jax
import jax.numpy as jnp
from jax import lax
from jax.sharding import PartitionSpec as P

SPAN = 256
INNER = 4096


def sent_together(arrays, axis, dim, along):
    columns = [a.reshape(*a.shape[:along], -1) for a in arrays]
    both = jnp.concatenate(columns, axis=along)
    whole, at, done = (lax.all_gather(both, axis, axis=dim, tiled=True), 0, [])
    for a, column in zip(arrays, columns):
        slab = whole[..., at : at + column.shape[along]]
        done.append(slab.reshape(*slab.shape[:along], *a.shape[along:]))
        at += column.shape[along]
    return tuple(done)


def copy_for_each(value, axis):
    copies = jnp.broadcast_to(value, (lax.axis_size(axis), *value.shape))
    return lax.all_to_all(copies, axis, split_axis=0, concat_axis=0, tiled=True)


def taken_together(value, axis):
    everything = copy_for_each(value, axis)
    return jnp.sum(everything, axis=0)


def local_scan(blocks_x, b_rows, c_rows, steps_here, decay_rates):
    cumlog = jnp.cumsum(-decay_rates[None, :, None] * steps_here, axis=2)
    scores = jnp.einsum("cqn,csn->cqs", c_rows, b_rows, preferred_element_type=jnp.float32)
    lower_mask = jnp.tril(jnp.ones((SPAN, SPAN), dtype=bool))
    log_gaps = cumlog[:, :, :, None] - cumlog[:, :, None, :]
    decays = jnp.where(lower_mask, jnp.exp(jnp.where(lower_mask, log_gaps, 0.0)), 0.0)
    weights = (scores[:, None] * decays * steps_here[:, :, None, :]).astype(jnp.bfloat16)
    intra_out = jnp.einsum("chts,cshp->cthp", weights, blocks_x, preferred_element_type=jnp.float32)
    end_logs = cumlog[:, :, -1]
    in_weights = jnp.exp(end_logs[:, :, None] - cumlog) * steps_here
    b_weighted = (b_rows[:, None].astype(jnp.float32) * in_weights[..., None]).astype(jnp.bfloat16)
    block_states = jnp.einsum(
        "cshp,chsn->chpn", blocks_x, b_weighted, preferred_element_type=jnp.float32
    )

    def advance(carried, inputs):
        gain_log, block_state = inputs
        return (jnp.exp(gain_log)[:, None, None] * carried + block_state, carried)

    initial = jnp.zeros(block_states.shape[1:], jnp.float32)
    end_state, entering = lax.scan(advance, initial, (end_logs, block_states))
    before = jnp.cumsum(end_logs, axis=0) - end_logs
    whole_decay = jnp.exp(jnp.sum(end_logs, axis=0))
    return ((intra_out, entering, cumlog, before, c_rows), (whole_decay, end_state))


def finish(pieces, carried):
    intra_out, entering, cumlog, before, c_rows = pieces
    states = entering + jnp.exp(before)[:, :, None, None] * carried[None]
    inter = jnp.einsum("ctn,chpn->cthp", c_rows.astype(jnp.float32), states)
    inter = inter * jnp.exp(cumlog).transpose(0, 2, 1)[..., None]
    outputs = intra_out + inter
    return outputs.reshape(outputs.shape[0] * outputs.shape[1], -1)


def body(
    ssm_input,
    gate_z,
    proj_forward,
    proj_backward,
    step_raw,
    head_params,
    skip_gain,
    norm_gain,
    out_weight,
):
    frames, inner_here = ssm_input.shape
    heads_here = step_raw.shape[1]
    width = inner_here // heads_here
    blocks = frames // SPAN
    shape_x = (blocks, SPAN, heads_here, width)
    shape_rows = (blocks, SPAN, proj_forward.shape[2])

    def to_blocks(steps):
        return steps.reshape(heads_here, blocks, SPAN).transpose(1, 0, 2)

    steps_fwd = jax.nn.softplus(step_raw[0] + head_params[0, 1][:, None])
    steps_bwd = jax.nn.softplus(step_raw[1] + head_params[1, 1][:, None])[:, ::-1]
    fwd_parts, fwd_end = local_scan(
        ssm_input.reshape(shape_x),
        proj_forward[0].reshape(shape_rows),
        proj_forward[1].reshape(shape_rows),
        to_blocks(steps_fwd),
        head_params[0, 0],
    )
    bwd_parts, bwd_end = local_scan(
        ssm_input[::-1].reshape(shape_x),
        proj_backward[0][::-1].reshape(shape_rows),
        proj_backward[1][::-1].reshape(shape_rows),
        to_blocks(steps_bwd),
        head_params[1, 0],
    )
    decays_all, states_all = tuple(
        (
            part.astype(jnp.float32)
            for part in sent_together(
                (
                    jnp.stack([fwd_end[0], bwd_end[0]])[None].astype(jnp.bfloat16),
                    jnp.stack([fwd_end[1], bwd_end[1]])[None].astype(jnp.bfloat16),
                ),
                "seq",
                0,
                3,
            )
        )
    )
    own_index = lax.axis_index("seq")
    group_size = lax.axis_size("seq")

    def accumulate(position, carried):
        forward_state, backward_state = carried
        mirror = group_size - 1 - position
        forward_state = jnp.where(
            position < own_index,
            decays_all[position, 0][:, None, None] * forward_state + states_all[position, 0],
            forward_state,
        )
        backward_state = jnp.where(
            mirror > own_index,
            decays_all[mirror, 1][:, None, None] * backward_state + states_all[mirror, 1],
            backward_state,
        )
        return (forward_state, backward_state)

    empty_state = jnp.zeros(fwd_end[1].shape, jnp.float32)
    carry_fwd, carry_bwd = lax.fori_loop(0, group_size, accumulate, (empty_state, empty_state))
    forward_out = finish(fwd_parts, carry_fwd)
    backward_out = finish(bwd_parts, carry_bwd)[::-1]
    skipped = (
        ssm_input.reshape(frames, heads_here, width).astype(jnp.float32) * skip_gain[:, None]
    ).reshape(frames, inner_here)
    gated = (forward_out + backward_out + skipped) * jax.nn.silu(gate_z.astype(jnp.float32))
    squares = taken_together(jnp.sum(gated * gated, axis=1), "chan")
    scale = lax.rsqrt(squares / INNER + 1.0)
    normed = (gated * scale[:, None] * norm_gain).astype(jnp.bfloat16)
    frame_share = lax.all_to_all(normed, "chan", split_axis=0, concat_axis=1, tiled=True)
    projected = jnp.dot(
        frame_share,
        lax.all_gather(out_weight, "chan", axis=1, tiled=True),
        preferred_element_type=jnp.float32,
    ).astype(jnp.bfloat16)
    return lax.all_to_all(projected, "chan", split_axis=1, concat_axis=0, tiled=True)


def solution(mesh):
    in_specs = (
        P(("batch", "seq"), "chan"),
        P(("batch", "seq"), "chan"),
        P(None, ("batch", "seq"), None),
        P(None, ("batch", "seq"), None),
        P(None, "chan", ("batch", "seq")),
        P(None, None, "chan"),
        P("chan"),
        P("chan"),
        P(None, "chan"),
    )
    out_specs = P(("batch", "seq"), "chan")
    return jax.shard_map(body, mesh=mesh, in_specs=in_specs, out_specs=out_specs, check_vma=False)
```

profile of v0, /device:TPU:96, one launch (start us, length us, event | category | flops | bytes accessed | tf_op | source)
XLA Modules:
  0.0 171.4 jit_solution(11320585137728651989)
XLA Ops:
  7.3 1.2 copy.167
  8.5 6.3 %rev.17 = bf16[1024,256]{1,0:T(8,128)(2,1)S(1)} reverse(bf16[1024,256]{1,0:T(8,128)(2,1)} %param.15), dimensions={0} | reverse | bytes 1048576 | tf_op jit(solution)/shard_map/rev | solution.py:97
  16.4 0.8 compare_select_fusion
  18.0 4.8 %reduce-window.14 = f32[4,4,2,128]{3,2,1,0:T(2,128)S(1)} reduce-window(f32[4,4,2,128]{3,2,1,0:T(2,128)S(1)} %reshape.296, f32[]{:T(128)} %constant.83.clone.1), window={size=1x1x1x128 pad=0_0x0_0x0_0x127_0}, to_apply=%region_0.1 | reduce-window | flops 520192 | bytes 32772 | tf_op jit(solution)/shard_map/reduce-window
  23.6 1.1 fusion.56
  24.8 1.2 reshape.298
  26.6 1.9 %convolution_bitcast_fusion.3 = f32[4,4,64,128]{3,2,1,0:T(8,128)S(1)} fusion(f32[4,4,256]{2,1,0:T(4,128)S(1)} %get-tuple-element.329, f32[4,256,128]{2,1,0:T(8,128)S(1)} %convert_element_type.76, bf16[4,256,4,64]{1,0,3,2:T(4,128)(2,1)} %reshape.298), kind=kOutput, calls=%fused_computation.48 | convolution fusion | flops 68157440 | bytes 1589248 | tf_op jit(solution)/shard_map/cshp,chsn->chpn/dot_general | solution.py:42
  29.3 4.8 %reduce-window.16 = f32[4,4,2,128]{3,2,1,0:T(2,128)S(1)} reduce-window(f32[4,4,2,128]{3,2,1,0:T(2,128)S(1)} %reshape.300, f32[]{:T(128)} %constant.83.clone.1), window={size=1x1x1x128 pad=0_0x0_0x0_0x127_0}, to_apply=%region_6.7 | reduce-window | flops 520192 | bytes 32772 | tf_op jit(solution)/shard_map/reduce-window.2
  34.9 1.8 %slice_bitcast_fusion = (bf16[1024,128]{1,0:T(8,128)(2,1)}, bf16[1024,128]{1,0:T(8,128)(2,1)S(1)}) fusion(bf16[2,1024,128]{2,1,0:T(8,128)(2,1)} %param.18), kind=kLoop, calls=%fused_computation.70 | loop fusion | bytes 1048576 | tf_op jit(solution)/shard_map/squeeze | solution.py:99
  36.9 0.8 convert_element_type.78
  39.3 2.0 %convolution_bitcast_fusion.2 = f32[4,4,64,128]{3,2,1,0:T(8,128)S(1)} fusion(bf16[4,256,4,64]{1,3,2,0:T(8,128)(2,1)S(1)} %copy.176, f32[4,4,256]{2,1,0:T(4,128)S(1)} %get-tuple-element.324, f32[4,256,128]{2,1,0:T(8,128)} %convert_element_type.78), kind=kOutput, calls=%fused_computation.47 | convolution fusion | flops 68157440 | bytes 1589248 | tf_op jit(solution)/shard_map/cshp,chsn->chpn/dot_general | solution.py:42
  42.7 2.0 %all_gather.6 = bf16[2,2,4,8193]{3,2,1,0:T(4,128)(2,1)S(1)} all-gather(bf16[1,2,4,8193]{3,2,1,0:T(4,128)(2,1)S(1)} %maximum_maximum_fusion), channel_id=1, replica_groups=mesh['seq'=2,'chan'=16,'batch'=8] {'seq'}, dimensions={0}, use_global_device_ids=true | all-gather | bytes 393264 | tf_op jit(solution)/shard_map/all_gather | solution.py:13
  45.4 3.2 %rev.18 = bf16[1024,128]{1,0:T(8,128)(2,1)S(1)} reverse(bf16[1024,128]{1,0:T(8,128)(2,1)} %get-tuple-element.319), dimensions={0} | reverse | bytes 524288 | tf_op jit(solution)/shard_map/rev | solution.py:99
  49.6 3.1 %fusion.22 = f32[4,256,4,64]{1,3,2,0:T(8,128)} fusion(bf16[4,256,4,64]{1,3,2,0:T(8,128)(2,1)S(1)} %copy.176, f32[4,4,256]{2,1,0:T(4,128)} %bitcast.166, f32[4,4,256]{2,1,0:T(4,128)S(1)} %copy-done.9, f32[4,256,256]{2,1,0:T(8,128)S(1)} %fusion.58, pred[256,256]{1,0:T(8,128)(4,1)S(1)} %iota_compare_fusion), kind=kOutput, calls=%fused_computation.37 | convolution fusion | flops 140509184 | bytes 2719744 | tf_op jit(solution)/shard_map/chts,cshp->cthp/dot_general | solution.py:38
  53.8 1.6 fusion.25
  56.3 1.5 rev.19
  58.2 2.5 %fusion.23 = f32[4,256,4,64]{1,3,2,0:T(8,128)S(1)} fusion(f32[4,4,256]{2,1,0:T(4,128)S(1)} %copy-done.13, f32[4,4,256]{2,1,0:T(4,128)S(1)} %copy-done.7, f32[4,256,256]{2,1,0:T(8,128)S(1)} %fusion.57, pred[256,256]{1,0:T(8,128)(4,1)S(1)} %copy-done.11, bf16[4,256,4,64]{1,0,3,2:T(4,128)(2,1)} %reshape.298), kind=kOutput, calls=%fused_computation.38 | convolution fusion | flops 140509184 | bytes 2719744 | tf_op jit(solution)/shard_map/chts,cshp->cthp/dot_general | solution.py:38
  61.8 1.2 copy.198
  63.3 1.8 %multiply_reduce_fusion = (f32[1024]{0:T(1024)S(1)}, f32[1024,256]{0,1:T(8,128)S(1)}) fusion(bf16[1024,256]{0,1:T(8,128)(2,1)S(1)} %copy.182, f32[256]{0:T(256)S(1)} %mul.274, bf16[1024,256]{0,1:T(8,128)(2,1)S(1)} %copy.167, f32[1024,256]{0,1:T(8,128)} %bitcast.150, f32[1024,256]{0,1:T(8,128)S(1)} %rev.19), kind=kLoop, calls=%fused_computation.55 | loop fusion | flops 3144704 | bytes 4199424 | tf_op jit(solution)/shard_map/reduce_sum | solution.py:143
  65.2 15.2 %all_to_all.46 = f32[16,1,1024]{2,1,0:T(1,128)S(1)} all-to-all(f32[16,1,1024]{2,1,0:T(1,128)S(1)} %broadcast_in_dim.57), channel_id=1, replica_groups=mesh['seq'=2,'chan'=16,'batch'=8] {'chan'}, dimensions={0} | all-to-all | bytes 131072 | tf_op jit(solution)/shard_map/all_to_all | solution.py:23
  80.8 18.8 %all_to_all.44 = bf16[16,64,256]{2,1,0:T(8,128)(2,1)S(1)} all-to-all(bf16[16,64,256]{2,1,0:T(8,128)(2,1)S(1)} %bitcast.160), channel_id=1, replica_groups=mesh['seq'=2,'chan'=16,'batch'=8] {'chan'}, dimensions={0} | all-to-all | bytes 1048576 | tf_op jit(solution)/shard_map/all_to_all | solution.py:146
  99.7 42.4 %all-gather.2.cloned.1.call-done = bf16[4096,2048]{1,0:T(8,128)(2,1)} async-done(((bf16[4096,128]{1,0:T(8,128)(2,1)}), bf16[4096,2048]{1,0:T(8,128)(2,1)}) %all-gather.2.cloned.1.call-update) | async-done | bytes 16777232 | tf_op jit(solution)/shard_map/all_gather | solution.py:149
  142.1 8.8 %fusion.28 = bf16[8,16,8,128]{3,2,1,0:T(8,128)(2,1)S(1)} fusion(bf16[64,4096]{1,0:T(8,128)(2,1)S(1)} %bitcast.151, bf16[4096,2048]{1,0:T(8,128)(2,1)} %all-gather.2.cloned.1.call-done), kind=kOutput, calls=%fused_computation.49 | convolution fusion | flops 1073872896 | bytes 17563648 | tf_op jit(solution)/shard_map/dot_general | solution.py:147
  150.9 12.9 %all_to_all.45 = bf16[64,16,128]{2,0,1:T(8,128)(2,1)S(1)} all-to-all(bf16[64,16,128]{2,0,1:T(8,128)(2,1)S(1)} %bitcast.162), channel_id=1, replica_groups=mesh['seq'=2,'chan'=16,'batch'=8] {'chan'}, dimensions={1} | all-to-all | bytes 524288 | tf_op jit(solution)/shard_map/all_to_all | solution.py:152
  (143 shorter events, 16.7 us)
Async XLA Ops:
  6.5 135.5 %all-gather.2.cloned.1.call-start = ((), (), s32[]{:S(2)}) async-start(), calls=%async_computation.3 | async-start | bytes 17825792 | tf_op jit(solution)/shard_map/all_gather | solution.py:149
  17.9 20.8 %copy-start.5 = (f32[4,1024]{1,0:T(4,128)}, f32[4,1024]{1,0:T(4,128)S(1)}, u32[]{:S(2)}) copy-start(f32[4,1024]{1,0:T(4,128)S(1)} %rev.15) | copy-start | bytes 49156
  18.0 10.6 %copy-start.12 = (f32[4,4,256]{2,1,0:T(4,128)}, f32[4,4,256]{2,1,0:T(4,128)S(1)}, u32[]{:S(2)}) copy-start(f32[4,4,256]{2,1,0:T(4,128)S(1)} %get-tuple-element.314) | copy-start | bytes 49156
  23.3 3.3 %copy-start.6 = (f32[4,4,256]{2,1,0:T(4,128)}, f32[4,4,256]{2,1,0:T(4,128)S(1)}, u32[]{:S(2)}) copy-start(f32[4,4,256]{2,1,0:T(4,128)S(1)} %reduce_window_sum.59) | copy-start | bytes 49156
  29.2 7.5 %copy-start = (f32[4,4,64,128]{3,2,1,0:T(8,128)}, f32[4,4,64,128]{3,2,1,0:T(8,128)S(1)}, u32[]{:S(2)}) copy-start(f32[4,4,64,128]{3,2,1,0:T(8,128)S(1)} %get-tuple-element.216) | copy-start | bytes 1572868
  29.2 7.7 %copy-start.16 = (f32[4,4]{1,0:T(4,128)}, f32[4,4]{1,0:T(4,128)S(1)}, u32[]{:S(2)}) copy-start(f32[4,4]{1,0:T(4,128)S(1)} %get-tuple-element.516) | copy-start | bytes 196
  34.6 6.8 %copy-start.8 = (f32[4,4,256]{2,1,0:T(4,128)}, f32[4,4,256]{2,1,0:T(4,128)S(1)}, u32[]{:S(2)}) copy-start(f32[4,4,256]{2,1,0:T(4,128)S(1)} %reduce_window_sum.62) | copy-start | bytes 49156
  42.0 0.8 copy-start.2
  42.0 7.6 %copy-start.9 = (f32[4,4,256]{2,1,0:T(4,128)S(1)}, f32[4,4,256]{2,1,0:T(4,128)}, u32[]{:S(2)}) copy-start(f32[4,4,256]{2,1,0:T(4,128)} %copy-done.8) | copy-start | bytes 49156
  48.7 4.1 %copy-start.10 = (pred[256,256]{1,0:T(8,128)(4,1)}, pred[256,256]{1,0:T(8,128)(4,1)S(1)}, u32[]{:S(2)}) copy-start(pred[256,256]{1,0:T(8,128)(4,1)S(1)} %iota_compare_fusion) | copy-start | bytes 196612
  52.7 1.0 copy-start.3
  52.7 1.0 copy-start.15
  55.3 2.4 %copy-start.17 = (f32[4,4]{1,0:T(4,128)S(1)}, f32[4,4]{1,0:T(4,128)}, u32[]{:S(2)}) copy-start(f32[4,4]{1,0:T(4,128)} %copy-done.16) | copy-start | bytes 196
  55.3 2.8 %copy-start.7 = (f32[4,4,256]{2,1,0:T(4,128)S(1)}, f32[4,4,256]{2,1,0:T(4,128)}, u32[]{:S(2)}) copy-start(f32[4,4,256]{2,1,0:T(4,128)} %copy-done.6) | copy-start | bytes 49156
  55.4 2.8 %copy-start.11 = (pred[256,256]{1,0:T(8,128)(4,1)S(1)}, pred[256,256]{1,0:T(8,128)(4,1)}, u32[]{:S(2)}) copy-start(pred[256,256]{1,0:T(8,128)(4,1)} %copy-done.10) | copy-start | bytes 196612
  55.4 2.8 %copy-start.13 = (f32[4,4,256]{2,1,0:T(4,128)S(1)}, f32[4,4,256]{2,1,0:T(4,128)}, u32[]{:S(2)}) copy-start(f32[4,4,256]{2,1,0:T(4,128)} %copy-done.12) | copy-start | bytes 49156
  58.2 2.5 %copy-start.1 = (f32[4,4,64,128]{3,2,1,0:T(8,128)S(1)}, f32[4,4,64,128]{3,2,1,0:T(8,128)}, u32[]{:S(2)}) copy-start(f32[4,4,64,128]{3,2,1,0:T(8,128)} %copy-done) | copy-start | bytes 1572868
  58.2 2.5 %copy-start.14 = (f32[4,256,4]{1,2,0:T(4,128)S(1)}, f32[4,256,4]{1,2,0:T(4,128)}, u32[]{:S(2)}) copy-start(f32[4,256,4]{1,2,0:T(4,128)} %get-tuple-element.330) | copy-start | bytes 49156
  60.7 2.3 %copy-start.4 = (bf16[1024,256]{1,0:T(8,128)(2,1)S(1)}, bf16[1024,256]{1,0:T(8,128)(2,1)}, u32[]{:S(2)}) copy-start(bf16[1024,256]{1,0:T(8,128)(2,1)} %param.16) | copy-start | bytes 1572868
  60.7 2.5 %copy-start.19 = (f32[4]{0:T(128)S(1)}, f32[4]{0:T(128)}, u32[]{:S(2)}) copy-start(f32[4]{0:T(128)} %param.21) | copy-start | bytes 52
  61.8 18.7 %copy-start.18 = (f32[256]{0:T(256)S(1)}, f32[256]{0:T(256)}, u32[]{:S(2)}) copy-start(f32[256]{0:T(256)} %param.22) | copy-start | bytes 3076
Sparse Core Ops, SparseCore 0:
  9.7 132.2 all-gather.1
where the time goes:
time: 173 us; the launch traced here: 171 us
  blocking collectives  48.9 us (28%)
  waiting for transfers between devices  43.1 us (25%)
  local copies, waits for them, and re-layouts  26 us (15%)
  matrix products  20.8 us (12%)
  other arithmetic  18.2 us (11%)
  between operations  14 us (8%)
    all_gather x1, waiting for transfers between devices, body(): lax.all_gather(out_weight, 'chan', axis=1, tiled=True)  42.4 us
    all_to_all x1, blocking collectives, body(): lax.all_to_all(normed, 'chan', split_axis=0, concat_axis=1, tiled=True)  18.8 us
    all_to_all x1, blocking collectives, copy_for_each(): return lax.all_to_all(copies, axis, split_axis=0, concat_axis=0, tiled=True)  15.2 us
    all_to_all x1, blocking collectives, body(): lax.all_to_all(projected, 'chan', split_axis=1, concat_axis=0, tiled=True)  12.9 us
    another operation x8, other arithmetic  9.88 us
    dot_general x1, matrix products, body(): jnp.dot(frame_share, lax.all_gather(out_weight, 'chan', axis=1, tiled=Tru...  8.79 us
    rev x1, local copies, waits for them, and re-layouts, body(): ssm_input[::-1].reshape(shape_x)  6.33 us
    dot_general x2, matrix products, local_scan(): jnp.einsum('chts,cshp->cthp', weights, blocks_x, preferred_element_type=j...  5.62 us
  transfers between devices with their start and end apart: 1, of which 1 were waited for; matrix products, arithmetic and copies ran while one was open for 32% of the time, Pallas kernels for 0%

commit v1 on v0

--- a/solution.py
+++ b/solution.py
@@ -146,7 +146,7 @@
     frame_share = lax.all_to_all(normed, "chan", split_axis=0, concat_axis=1, tiled=True)
     projected = jnp.dot(
         frame_share,
-        lax.all_gather(out_weight, "chan", axis=1, tiled=True),
+        jnp.concatenate(lax.all_gather(out_weight, "chan"), axis=1),
         preferred_element_type=jnp.float32,
     ).astype(jnp.bfloat16)
     return lax.all_to_all(projected, "chan", split_axis=1, concat_axis=0, tiled=True)

time: 173 us -> 190 us (1.098)
  local copies, waits for them, and re-layouts: 26 us -> 43.3 us
  waiting for transfers between devices: 43.1 us -> 37.8 us
  blocking collectives: 48.9 us -> 52 us
    reshape x1 -> x2, local copies, waits for them, and re-layouts: 0.02 us -> 20.8 us  [the longest x1 20.8 us: body(): jnp.concatenate(lax.all_gather(out_weight, 'chan'), axis=1)]
    all_gather x1, waiting for transfers between devices: 42.4 us -> 37.1 us  [body(): lax.all_gather(out_weight, 'chan')]
    rev x1, local copies, waits for them, and re-layouts: 3.17 us -> 0.28 us  [body(): proj_backward[1][::-1].reshape(shape_rows)]
    dot_general x1, matrix products: 8.79 us -> 11 us  [body(): jnp.dot(frame_share, jnp.concatenate(lax.all_gather(out_weight, 'chan'),...]
    all_to_all x1, blocking collectives: 18.8 us -> 20.8 us  [body(): lax.all_to_all(normed, 'chan', split_axis=0, concat_axis=1, tiled=True)]
    unnamed x47 -> x37, local copies, waits for them, and re-layouts: 4.97 us -> 4.15 us
  transfers between devices with their start and end apart: 1 -> 1, of which waited for: 1 -> 1; matrix products, arithmetic and copies ran while one was open for 32% -> 27% of each run, Pallas kernels for 0% -> 0%
where the time goes in v1:
time: 190 us; the launch traced here: 187 us
  blocking collectives  52 us (27%)
  local copies, waits for them, and re-layouts  43.3 us (23%)
  waiting for transfers between devices  37.8 us (20%)
  matrix products  21.3 us (11%)
  other arithmetic  18.5 us (10%)
  between operations  13.9 us (7%)
    all_gather x1, waiting for transfers between devices, body(): lax.all_gather(out_weight, 'chan')  37.1 us
    all_to_all x1, blocking collectives, body(): lax.all_to_all(normed, 'chan', split_axis=0, concat_axis=1, tiled=True)  20.8 us
    reshape x1, local copies, waits for them, and re-layouts, body(): jnp.concatenate(lax.all_gather(out_weight, 'chan'), axis=1)  20.8 us
    all_to_all x1, blocking collectives, copy_for_each(): return lax.all_to_all(copies, axis, split_axis=0, concat_axis=0, tiled=True)  15.3 us
    all_to_all x1, blocking collectives, body(): lax.all_to_all(projected, 'chan', split_axis=1, concat_axis=0, tiled=True)  13.7 us
    dot_general x1, matrix products, body(): jnp.dot(frame_share, jnp.concatenate(lax.all_gather(out_weight, 'chan'),...  11 us
    another operation x8, other arithmetic  9.89 us
    rev x1, local copies, waits for them, and re-layouts, body(): ssm_input[::-1].reshape(shape_x)  6.33 us
  transfers between devices with their start and end apart: 1, of which 1 were waited for; matrix products, arithmetic and copies ran while one was open for 27% of the time, Pallas kernels for 0%

profile of v1, /device:TPU:96, one launch (start us, length us, event | category | flops | bytes accessed | tf_op | source)
XLA Modules:
  0.0 187.3 jit_solution(7060594338572278767)
XLA Ops:
  7.3 1.3 copy.172
  8.6 6.3 %rev.17 = bf16[1024,256]{1,0:T(8,128)(2,1)S(1)} reverse(bf16[1024,256]{1,0:T(8,128)(2,1)} %param.15), dimensions={0} | reverse | bytes 1048576 | tf_op jit(solution)/shard_map/rev | solution.py:97
  17.1 0.8 negate_bitcast_fusion
  17.8 0.8 compare_select_fusion
  19.5 4.8 %reduce-window.14 = f32[4,4,2,128]{3,2,1,0:T(2,128)S(1)} reduce-window(f32[4,4,2,128]{3,2,1,0:T(2,128)S(1)} %reshape.302, f32[]{:T(128)} %constant.83.clone.1), window={size=1x1x1x128 pad=0_0x0_0x0_0x127_0}, to_apply=%region_0.1 | reduce-window | flops 520192 | bytes 32772 | tf_op jit(solution)/shard_map/reduce-window
  25.1 4.8 %reduce-window.16 = f32[4,4,2,128]{3,2,1,0:T(2,128)S(1)} reduce-window(f32[4,4,2,128]{3,2,1,0:T(2,128)S(1)} %reshape.306, f32[]{:T(128)} %constant.83.clone.1), window={size=1x1x1x128 pad=0_0x0_0x0_0x127_0}, to_apply=%region_6.7 | reduce-window | flops 520192 | bytes 32772 | tf_op jit(solution)/shard_map/reduce-window.2
  30.8 1.2 reshape.304
  32.0 1.0 copy.187
  35.5 1.8 convolution_bitcast_fusion.3
  38.1 1.2 slice_bitcast_fusion
  41.2 1.0 convolution_bitcast_fusion.2
  43.0 2.1 %all_gather.9 = bf16[2,2,4,8193]{3,2,1,0:T(4,128)(2,1)} all-gather(bf16[1,2,4,8193]{3,2,1,0:T(4,128)(2,1)S(1)} %maximum_maximum_fusion), channel_id=1, replica_groups=mesh['seq'=2,'chan'=16,'batch'=8] {'seq'}, dimensions={0}, use_global_device_ids=true | all-gather | bytes 393264 | tf_op jit(solution)/shard_map/all_gather | solution.py:13
  45.2 1.2 slice_convert_fusion
  46.7 0.8 convert_reduce_fusion
  48.5 2.5 %fusion.22 = f32[4,256,4,64]{1,3,2,0:T(8,128)} fusion(bf16[4,256,4,64]{1,3,2,0:T(8,128)(2,1)S(1)} %copy.181, f32[4,4,256]{2,1,0:T(4,128)S(1)} %bitcast.172, f32[4,4,256]{2,1,0:T(4,128)S(1)} %reduce_window_sum.62, f32[4,256,256]{2,1,0:T(8,128)S(1)} %fusion.58, pred[256,256]{1,0:T(8,128)(4,1)S(1)} %iota_compare_fusion), kind=kOutput, calls=%fused_computation.37 | convolution fusion | flops 140509184 | bytes 2719744 | tf_op jit(solution)/shard_map/chts,cshp->cthp/dot_general | solution.py:38
  51.7 1.6 fusion.25
  54.2 1.5 rev.19
  56.0 2.5 %fusion.23 = f32[4,256,4,64]{1,3,2,0:T(8,128)S(1)} fusion(f32[4,4,256]{2,1,0:T(4,128)S(1)} %get-tuple-element.314, f32[4,4,256]{2,1,0:T(4,128)S(1)} %reduce_window_sum.59, f32[4,256,256]{2,1,0:T(8,128)S(1)} %fusion.57, pred[256,256]{1,0:T(8,128)(4,1)S(1)} %iota_compare_fusion, bf16[4,256,4,64]{1,0,3,2:T(4,128)(2,1)} %reshape.304), kind=kOutput, calls=%fused_computation.38 | convolution fusion | flops 140509184 | bytes 2719744 | tf_op jit(solution)/shard_map/chts,cshp->cthp/dot_general | solution.py:38
  60.5 15.3 %all_to_all.46 = f32[16,1,1024]{2,1,0:T(1,128)S(1)} all-to-all(f32[16,1,1024]{2,1,0:T(1,128)S(1)} %broadcast_in_dim.57), channel_id=1, replica_groups=mesh['seq'=2,'chan'=16,'batch'=8] {'chan'}, dimensions={0} | all-to-all | bytes 131072 | tf_op jit(solution)/shard_map/all_to_all | solution.py:23
  76.2 20.8 %all_to_all.44 = bf16[16,64,256]{2,1,0:T(8,128)(2,1)S(1)} all-to-all(bf16[16,64,256]{2,1,0:T(8,128)(2,1)S(1)} %bitcast.166), channel_id=1, replica_groups=mesh['seq'=2,'chan'=16,'batch'=8] {'chan'}, dimensions={0} | all-to-all | bytes 1048576 | tf_op jit(solution)/shard_map/all_to_all | solution.py:146
  97.1 37.1 %all-gather.3.cloned.1.call-done = bf16[65536,128]{1,0:T(8,128)(2,1)} async-done(((bf16[4096,128]{1,0:T(8,128)(2,1)}), bf16[65536,128]{1,0:T(8,128)(2,1)}) %all-gather.3.cloned.1.call-update) | async-done | bytes 16777232 | tf_op jit(solution)/shard_map/all_gather | solution.py:149
  134.2 20.8 %copy.191 = bf16[4096,16,128]{0,2,1:T(8,128)(2,1)} copy(bf16[4096,16,128]{2,0,1:T(8,128)(2,1)} %bitcast.152) | data formatting | bytes 33554432 | tf_op jit(solution)/shard_map/reshape | solution.py:149
  155.0 11.0 %fusion.28 = bf16[8,16,8,128]{3,2,1,0:T(8,128)(2,1)S(1)} fusion(bf16[64,4096]{1,0:T(8,128)(2,1)S(1)} %bitcast.165, bf16[4096,2048]{0,1:T(8,128)(2,1)} %bitcast.151), kind=kOutput, calls=%fused_computation.49 | convolution fusion | flops 1073872896 | bytes 17563648 | tf_op jit(solution)/shard_map/dot_general | solution.py:147
  166.0 13.7 %all_to_all.45 = bf16[64,16,128]{2,0,1:T(8,128)(2,1)S(1)} all-to-all(bf16[64,16,128]{2,0,1:T(8,128)(2,1)S(1)} %bitcast.168), channel_id=1, replica_groups=mesh['seq'=2,'chan'=16,'batch'=8] {'chan'}, dimensions={1} | all-to-all | bytes 524288 | tf_op jit(solution)/shard_map/all_to_all | solution.py:152
  (134 shorter events, 18.5 us)
Async XLA Ops:
  6.5 25.5 %copy-start.6 = (bf16[1024,256]{1,0:T(8,128)(2,1)S(1)}, bf16[1024,256]{1,0:T(8,128)(2,1)}, u32[]{:S(2)}) copy-start(bf16[1024,256]{1,0:T(8,128)(2,1)} %param.16) | copy-start | bytes 1572868
  6.5 127.7 %all-gather.3.cloned.1.call-start = ((), (), s32[]{:S(2)}) async-start(), calls=%async_computation.3 | async-start | bytes 17825792 | tf_op jit(solution)/shard_map/all_gather | solution.py:149
  7.3 26.8 %copy-start.7 = (bf16[2,1024,128]{2,1,0:T(8,128)(2,1)S(1)}, bf16[2,1024,128]{2,1,0:T(8,128)(2,1)}, u32[]{:S(2)}) copy-start(bf16[2,1024,128]{2,1,0:T(8,128)(2,1)} %param.17) | copy-start | bytes 1572868
  34.8 5.1 %copy-start = (bf16[1,1024,128]{2,1,0:T(8,128)(2,1)}, bf16[1,1024,128]{2,1,0:T(8,128)(2,1)S(1)}, u32[]{:S(2)}) copy-start(bf16[1,1024,128]{2,1,0:T(8,128)(2,1)S(1)} %get-tuple-element.321) | copy-start | bytes 786436
  38.0 3.1 %copy-start.3 = (f32[4,4,64,128]{3,2,1,0:T(8,128)}, f32[4,4,64,128]{3,2,1,0:T(8,128)S(1)}, u32[]{:S(2)}) copy-start(f32[4,4,64,128]{3,2,1,0:T(8,128)S(1)} %get-tuple-element.216) | copy-start | bytes 1572868
  38.0 4.2 %copy-start.9 = (f32[4,4]{1,0:T(4,128)}, f32[4,4]{1,0:T(4,128)S(1)}, u32[]{:S(2)}) copy-start(f32[4,4]{1,0:T(4,128)S(1)} %get-tuple-element.516) | copy-start | bytes 196
  42.8 3.9 %copy-start.11 = (f32[4,4]{1,0:T(4,128)}, f32[4,4]{1,0:T(4,128)S(1)}, u32[]{:S(2)}) copy-start(f32[4,4]{1,0:T(4,128)S(1)} %get-tuple-element.517) | copy-start | bytes 196
  50.9 0.7 copy-start.8
  51.6 4.0 %copy-start.10 = (f32[4,4]{1,0:T(4,128)S(1)}, f32[4,4]{1,0:T(4,128)}, u32[]{:S(2)}) copy-start(f32[4,4]{1,0:T(4,128)} %copy-done.9) | copy-start | bytes 196
  51.6 4.1 %copy-start.12 = (f32[4,4]{1,0:T(4,128)S(1)}, f32[4,4]{1,0:T(4,128)}, u32[]{:S(2)}) copy-start(f32[4,4]{1,0:T(4,128)} %reduce_window_sum.60) | copy-start | bytes 196
  51.6 4.1 %copy-start.1 = (bf16[1,1024,128]{2,1,0:T(8,128)(2,1)S(1)}, bf16[1,1024,128]{2,1,0:T(8,128)(2,1)}, u32[]{:S(2)}) copy-start(bf16[1,1024,128]{2,1,0:T(8,128)(2,1)} %copy-done) | copy-start | bytes 786436
  51.6 4.1 %copy-start.2 = (bf16[1,1024,128]{2,1,0:T(8,128)(2,1)S(1)}, bf16[1,1024,128]{2,1,0:T(8,128)(2,1)}, u32[]{:S(2)}) copy-start(bf16[1,1024,128]{2,1,0:T(8,128)(2,1)} %get-tuple-element.322) | copy-start | bytes 786436
  56.0 2.5 %copy-start.4 = (f32[4,4,64,128]{3,2,1,0:T(8,128)S(1)}, f32[4,4,64,128]{3,2,1,0:T(8,128)}, u32[]{:S(2)}) copy-start(f32[4,4,64,128]{3,2,1,0:T(8,128)} %copy-done.3) | copy-start | bytes 1572868
  58.5 1.3 copy-start.5
  58.5 1.3 copy-start.13
  58.9 17.0 %copy-start.14 = (f32[256]{0:T(256)S(1)}, f32[256]{0:T(256)}, u32[]{:S(2)}) copy-start(f32[256]{0:T(256)} %param.22) | copy-start | bytes 3076
Sparse Core Ops, SparseCore 0:
  9.8 124.4 all-gather.2
